TPU v7x, 128 devices: a whole 4x4x4 slice. The times are simulated.
128 devices in a mesh: dp: 16 (over y_hi, x, core), tensor: 8 (over z, y_lo).
Axes of the slice: x: 4, y: 4 (y_hi: 2, y_lo: 2; y = y_hi * 2 + y_lo), z: 4, core: 2. Of those that a mesh axis runs over, the one named last changes fastest.
Arguments:
- tokens: bfloat16 [32768, 1024], P(('dp', 'tensor')), may hold values from -6 to 6
- upstream: bfloat16 [32768, 1024], P(('dp', 'tensor')), may hold values from -6 to 6
- counts: int32 [512], P('dp'), may hold values from 37 to 49, as said below
- norm_gain: float32 [1024], replicated, may hold values from 0.5 to 1.5
- norm_bias: float32 [1024], replicated, may hold values from -4 to 4
- w_qkv: bfloat16 [1024, 3072], P('dp', 'tensor'), may hold values from -0.1875 to 0.1875
- w_out: bfloat16 [1024, 1024], P('tensor', 'dp'), may hold values from -0.1875 to 0.1875
Outputs:
- grad_tokens: bfloat16 [32768, 1024], P(('dp', 'tensor'))
- grad_qkv: float32 [1024, 3072], P('dp', 'tensor')
- grad_out: float32 [1024, 1024], P('tensor', 'dp')
- grad_gain: float32 [1024], replicated
- grad_bias: float32 [1024], replicated
Inputs may be any that keep to these rules, and one draw needn't show every extreme that they name: counts[i] is the number of visible tokens of image i, held in its first slots; some image has 49 in every draw.
All inputs are finite; a program needn't handle non-finite values.
Results may differ from a plain program's by a relative error of at most 0.014.
Values may be sent and summed in bfloat16 or wider, within the bound.
No kernel may reach another device: no remote copies, remote signals or barrier semaphores. Data moves between devices by JAX's collectives and lax.ppermute only.
A program may use at most 64 MiB of HBM per device.

v0:
```python
import functools

import jax
import jax.numpy as jnp
from jax import lax
from jax.sharding import Mesh
from jax.sharding import PartitionSpec as P

HEAD = 64
CAP = 64
TENSOR = ("tensor_0", "tensor_1")
DP = ("dp_0", "dp_1", "dp_2")
DP_TENSOR = ("dp_0", "dp_1", "dp_2", "tensor_0", "tensor_1")


def laid_out(pieces, dim):
    pieces = jnp.moveaxis(pieces, 0, dim)
    lengths = pieces.shape
    return pieces.reshape(*lengths[:dim], lengths[dim] * lengths[dim + 1], *lengths[dim + 2 :])


def sent_to_all(value, axis):
    copies = jnp.broadcast_to(value, (lax.axis_size(axis), *value.shape))
    return lax.all_to_all(copies, axis, split_axis=0, concat_axis=0, tiled=True)


def gather_directly(value, axis, dim):
    return laid_out(sent_to_all(value, axis), dim)


def in_blocks(value, dim, devices):
    before, after = (value.shape[:dim], value.shape[dim + 1 :])
    return jnp.moveaxis(value.reshape(*before, devices, -1, *after), dim, 0)


def summed_on_arrival(value, axis, dim):
    pieces = in_blocks(value, dim, lax.axis_size(axis))
    arrived = lax.all_to_all(pieces, axis, split_axis=0, concat_axis=0, tiled=True)
    return arrived.astype(jnp.float32).sum(axis=0)


def by_axis(value, axes):
    return functools.reduce(lax.psum, axes, value)


def layer_norm(tokens, norm_gain, norm_bias):
    values = tokens.astype(jnp.float32)
    centre = jnp.mean(values, axis=-1, keepdims=True)
    shifted = values - centre
    variance = jnp.mean(shifted * shifted, axis=-1, keepdims=True)
    inverse_std = lax.rsqrt(variance + 1e-06)
    scaled = shifted * inverse_std
    normed = (scaled * norm_gain + norm_bias).astype(jnp.bfloat16)
    return (normed, scaled, inverse_std)


def on_device(tokens, upstream, counts, norm_gain, norm_bias, w_qkv, w_out):
    local_rows = tokens.shape[0]
    own_images = local_rows // CAP
    start_image = lax.axis_index(TENSOR) * own_images
    own_counts = lax.dynamic_slice_in_dim(counts, start_image, own_images)
    own_live = (
        (jnp.arange(CAP, dtype=jnp.int32)[None, :] < own_counts[:, None])
        .reshape(-1)
        .astype(jnp.float32)
    )
    normed, scaled, inverse_std = layer_norm(tokens, norm_gain, norm_bias)
    all_normed = gather_directly(normed, TENSOR, 0)
    qkv_cols = gather_directly(w_qkv, DP, 0)
    out_rows = gather_directly(w_out, DP, 1)
    all_upstream = gather_directly(upstream, TENSOR, 0)
    group_rows = all_normed.shape[0]
    images = group_rows // CAP
    local_heads = qkv_cols.shape[1] // (3 * HEAD)
    slot_live = jnp.arange(CAP, dtype=jnp.int32)[None, :] < counts[:, None]
    group_live = slot_live.reshape(-1).astype(jnp.bfloat16)
    masked = all_upstream * group_live[:, None]
    projected = jnp.dot(all_normed, qkv_cols, preferred_element_type=jnp.float32).astype(
        jnp.bfloat16
    )
    projected = projected.reshape(images, CAP, local_heads, 3, HEAD)
    query_rows = projected[:, :, :, 0]
    key_rows = projected[:, :, :, 1]
    value_rows = projected[:, :, :, 2]
    score_scale = 1.0 / HEAD**0.5
    scores = (
        jnp.einsum("bqhe,bkhe->bhqk", query_rows, key_rows, preferred_element_type=jnp.float32)
        * score_scale
    )
    scores = jnp.where(slot_live[:, None, None, :], scores, -1e30)
    probs = jax.nn.softmax(scores, axis=-1)
    probs_low = probs.astype(jnp.bfloat16)
    attended = jnp.einsum(
        "bhqk,bkhe->bqhe", probs_low, value_rows, preferred_element_type=jnp.float32
    )
    attended = attended.astype(jnp.bfloat16).reshape(group_rows, local_heads * HEAD)
    out_part = lax.dot_general(
        attended, masked, (((0,), (0,)), ((), ())), preferred_element_type=jnp.float32
    )
    grad_out = summed_on_arrival(out_part.astype(jnp.bfloat16), DP, 1)
    grad_att = lax.dot_general(
        masked, out_rows, (((1,), (1,)), ((), ())), preferred_element_type=jnp.float32
    )
    grad_att = grad_att.astype(jnp.bfloat16).reshape(images, CAP, local_heads, HEAD)
    grad_probs = jnp.einsum(
        "bqhe,bkhe->bhqk", grad_att, value_rows, preferred_element_type=jnp.float32
    )
    row_delta = jnp.sum(probs * grad_probs, axis=-1, keepdims=True)
    grad_scores = (probs * (grad_probs - row_delta) * score_scale).astype(jnp.bfloat16)
    grad_value = jnp.einsum(
        "bhqk,bqhe->bkhe", probs_low, grad_att, preferred_element_type=jnp.float32
    ).astype(jnp.bfloat16)
    grad_query = jnp.einsum(
        "bhqk,bkhe->bqhe", grad_scores, key_rows, preferred_element_type=jnp.float32
    ).astype(jnp.bfloat16)
    grad_key = jnp.einsum(
        "bhqk,bqhe->bkhe", grad_scores, query_rows, preferred_element_type=jnp.float32
    ).astype(jnp.bfloat16)
    grad_proj = jnp.stack([grad_query, grad_key, grad_value], axis=3).reshape(
        group_rows, 3 * local_heads * HEAD
    )
    qkv_part = lax.dot_general(
        all_normed, grad_proj, (((0,), (0,)), ((), ())), preferred_element_type=jnp.float32
    )
    grad_qkv = summed_on_arrival(qkv_part.astype(jnp.bfloat16), DP, 0)
    grad_normed = lax.psum_scatter(
        lax.dot_general(
            grad_proj, qkv_cols, (((1,), (1,)), ((), ())), preferred_element_type=jnp.float32
        ).astype(jnp.bfloat16),
        TENSOR,
        scatter_dimension=0,
        tiled=True,
    ).astype(jnp.float32)
    grad_gain, grad_bias = (
        by_axis(jnp.sum(grad_normed * scaled, axis=0), DP_TENSOR),
        by_axis(jnp.sum(grad_normed, axis=0), DP_TENSOR),
    )
    grad_scaled = grad_normed * norm_gain
    grad_ln = inverse_std * (
        grad_scaled
        - jnp.mean(grad_scaled, axis=-1, keepdims=True)
        - scaled * jnp.mean(grad_scaled * scaled, axis=-1, keepdims=True)
    )
    grad_tokens = (upstream.astype(jnp.float32) * own_live[:, None] + grad_ln).astype(jnp.bfloat16)
    return (grad_tokens, grad_qkv, grad_out, grad_gain, grad_bias)


def solution(mesh):
    finer = Mesh(
        mesh.devices.reshape(2, 4, 2, 4, 2), ("dp_0", "dp_1", "dp_2", "tensor_0", "tensor_1")
    )
    in_specs = (
        P(DP_TENSOR, None),
        P(DP_TENSOR, None),
        P(DP),
        P(),
        P(),
        P(DP, TENSOR),
        P(TENSOR, DP),
    )
    out_specs = (P(DP_TENSOR, None), P(DP, TENSOR), P(TENSOR, DP), P(), P())
    return jax.shard_map(
        on_device, mesh=finer, in_specs=in_specs, out_specs=out_specs, check_vma=False
    )
```

profile of v0, /device:TPU:0, one launch (start us, length us, event | category | flops | bytes accessed | tf_op | source)
XLA Modules:
  0.0 364.1 jit_solution(6722173262081360029)
XLA Ops:
  7.2 0.8 broadcast_in_dim.25
  8.0 16.3 %all_to_all.30 = bf16[16,128,64]{1,2,0:T(8,128)(2,1)S(1)} all-to-all(bf16[16,128,64]{1,2,0:T(8,128)(2,1)S(1)} %broadcast_in_dim.25), channel_id=1, replica_groups=mesh['dp_0'=2,'dp_1'=4,'dp_2'=2,'tensor_0'=4,'tensor_1'=2] {'dp_0','dp_1..., dimensions={0} | all-to-all | bytes 524288 | tf_op jit(solution)/shard_map/all_to_all | solution.py:24
  24.3 0.9 broadcast_in_dim.17
  25.2 18.3 %all_to_all.31 = bf16[16,64,384]{2,1,0:T(8,128)(2,1)} all-to-all(bf16[16,64,384]{2,1,0:T(8,128)(2,1)S(1)} %broadcast_in_dim.17), channel_id=1, replica_groups=mesh['dp_0'=2,'dp_1'=4,'dp_2'=2,'tensor_0'=4,'tensor_1'=2] {'dp_0','dp_1..., dimensions={0} | all-to-all | bytes 1572864 | tf_op jit(solution)/shard_map/all_to_all | solution.py:24
  43.5 2.5 broadcast_in_dim.24
  45.9 5.6 %all-to-all-start.2 = ((bf16[8,256,1024]{2,1,0:T(8,128)(2,1)}), bf16[8,256,1024]{2,1,0:T(8,128)(2,1)}, u32[]{:S(2)}, u32[]{:S(2)}) async-start(bf16[8,256,1024]{2,1,0:T(8,128)(2,1)} %broadcast_in_dim.24), calls=%async_computation.2 | async-start | bytes 8388608 | tf_op jit(solution)/shard_map/all_to_all | solution.py:24
  51.7 0.3 fusion.39
  52.3 48.7 %all-to-all-done.2 = bf16[8,256,1024]{2,1,0:T(8,128)(2,1)} async-done(((bf16[8,256,1024]{2,1,0:T(8,128)(2,1)}), bf16[8,256,1024]{2,1,0:T(8,128)(2,1)}, u32[]{:S(2)}, u32[]{:S(2)}) %all-to-all-start.2) | async-done | bytes 4194336 | tf_op jit(solution)/shard_map/all_to_all | solution.py:24
  101.0 2.5 broadcast_in_dim.16
  103.5 4.7 %all-to-all-start = ((bf16[8,256,1024]{2,1,0:T(8,128)(2,1)}), bf16[8,256,1024]{2,1,0:T(8,128)(2,1)}, u32[]{:S(2)}, u32[]{:S(2)}) async-start(bf16[8,256,1024]{2,1,0:T(8,128)(2,1)} %broadcast_in_dim.16), calls=%async_computation | async-start | bytes 8388608 | tf_op jit(solution)/shard_map/all_to_all | solution.py:24
  108.6 2.5 broadcast_multiply_fusion
  111.2 2.0 copy-done
  113.1 1.3 convolution_convert_fusion.2
  114.4 0.4 reshape.128
  114.8 2.1 copy.34
  116.9 39.8 %all-to-all-done = bf16[8,256,1024]{2,1,0:T(8,128)(2,1)} async-done(((bf16[8,256,1024]{2,1,0:T(8,128)(2,1)}), bf16[8,256,1024]{2,1,0:T(8,128)(2,1)}, u32[]{:S(2)}, u32[]{:S(2)}) %all-to-all-start) | async-done | bytes 4194336 | tf_op jit(solution)/shard_map/all_to_all | solution.py:24
  156.7 4.7 %convolution_convert_fusion.1 = bf16[2048,384]{1,0:T(8,128)(2,1)S(1)} fusion(bf16[2048,1024]{1,0:T(8,128)(2,1)} %bitcast, bf16[1024,384]{1,0:T(8,128)(2,1)} %bitcast.74), kind=kOutput, calls=%fused_computation.4 | convolution fusion | flops 1611399168 | bytes 6553600 | tf_op jit(solution)/shard_map/dot_general | solution.py:78
  161.4 4.8 %reshape.134 = bf16[32,64,2,3,64]{4,3,2,1,0:T(4,128)(2,1)} reshape(bf16[2048,384]{1,0:T(8,128)(2,1)S(1)} %convolution_convert_fusion.1) | data formatting | bytes 3145728 | tf_op jit(solution)/shard_map/reshape | solution.py:81
  166.2 12.1 %fusion.58 = (bf16[32,64,2,1,64]{4,3,2,1,0:T(2,128)(2,1)S(1)}, bf16[32,64,2,1,64]{4,3,2,1,0:T(2,128)(2,1)}, bf16[32,64,2,1,64]{4,3,2,1,0:T(2,128)(2,1)}) fusion(bf16[32,64,2,3,64]{4,3,2,1,0:T(4,128)(2,1)} %reshape.134), kind=kLoop, calls=%fused_computation.75 | loop fusion | bytes 3145728 | tf_op jit(solution)/shard_map/slice | solution.py:84
  178.3 1.8 fusion.50
  180.2 4.8 %fusion.59 = (f32[32,2,64]{2,1,0:T(2,128)S(1)}, f32[32,2,64,64]{2,3,1,0:T(8,128)}) fusion(pred[32,64]{1,0:T(8,128)(4,1)S(1)} %iota_compare_fusion, bf16[32,64,2,1,64]{4,3,2,1,0:T(2,128)(2,1)} %get-tuple-element.21, bf16[32,64,2,1,64]{4,3,2,1,0:T(2,128)(2,1)} %get-tuple-element.20), kind=kOutput, calls=%fused_computation.76 | convolution fusion | flops 34603072 | bytes 2115584 | tf_op jit(solution)/shard_map/sub | solution.py:91
  185.0 3.6 fusion.21
  188.6 6.1 %fusion.23 = bf16[32,64,2,1,64]{1,4,2,0,3:T(8,128)(2,1)} fusion(f32[32,2,64,64]{2,3,1,0:T(8,128)} %fusion.50, bf16[32,64,2,1,64]{4,3,2,1,0:T(2,128)(2,1)} %get-tuple-element.20, f32[32,2,64,64]{2,3,1,0:T(8,128)} %get-tuple-element.23, f32[32,2,64]{2,1,0:T(2,128)S(1)} %get-tuple-element.22), kind=kOutput, calls=%fused_computation.29 | convolution fusion | flops 35655744 | bytes 3162112 | tf_op jit(solution)/shard_map/bhqk,bqhe->bkhe/dot_general | solution.py:116
  194.6 6.1 %fusion.26 = bf16[32,64,2,1,64]{1,4,2,0,3:T(8,128)(2,1)} fusion(f32[32,2,64,64]{2,3,1,0:T(8,128)} %fusion.50, bf16[32,64,2,1,64]{4,3,2,1,0:T(2,128)(2,1)} %get-tuple-element.21, f32[32,2,64,64]{2,3,1,0:T(8,128)} %get-tuple-element.23, f32[32,2,64]{2,1,0:T(2,128)S(1)} %get-tuple-element.22), kind=kOutput, calls=%fused_computation.30 | convolution fusion | flops 35655744 | bytes 3162112 | tf_op jit(solution)/shard_map/bhqk,bkhe->bqhe/dot_general | solution.py:113
  200.7 2.6 pad_maximum_fusion
  203.3 3.8 %copy.36 = bf16[32,64,2,3,64]{1,0,4,3,2:T(8,128)(2,1)} copy(bf16[32,64,2,3,64]{1,4,2,0,3:T(8,128)(2,1)S(1)} %pad_maximum_fusion) | data formatting | bytes 3145728 | tf_op jit(solution)/shard_map/stack | solution.py:119
  207.1 5.6 %reshape.129 = bf16[2048,384]{0,1:T(8,128)(2,1)} reshape(bf16[32,64,2,3,64]{1,0,4,3,2:T(8,128)(2,1)} %copy.36) | data formatting | bytes 3145728 | tf_op jit(solution)/shard_map/reshape | solution.py:119
  212.7 6.0 %convolution_convert_fusion = bf16[2048,1024]{1,0:T(8,128)(2,1)} fusion(bf16[2048,384]{0,1:T(8,128)(2,1)} %reshape.129, bf16[1024,384]{1,0:T(8,128)(2,1)} %bitcast.75), kind=kOutput, calls=%fused_computation.2 | convolution fusion | flops 1612709888 | bytes 6553600 | tf_op jit(solution)/shard_map/dot_general | solution.py:127
  218.7 2.1 fusion.22
  220.8 0.7 copy.39
  221.5 0.8 reshape.131
  222.3 2.9 convolution_convert_fusion.6
  225.2 0.8 copy.40
  226.0 4.3 %all-to-all-start.5 = ((bf16[16,128,64]{1,2,0:T(8,128)(2,1)}), bf16[16,128,64]{1,2,0:T(8,128)(2,1)S(1)}, u32[]{:S(2)}, u32[]{:S(2)}) async-start(bf16[16,128,64]{1,2,0:T(8,128)(2,1)} %bitcast.17), calls=%async_computation.6 | async-start | bytes 524288 | tf_op jit(solution)/shard_map/all_to_all | solution.py:38
  230.4 6.0 %convolution_convert_fusion.5 = bf16[1024,384]{1,0:T(8,128)(2,1)} fusion(bf16[2048,1024]{1,0:T(8,128)(2,1)} %bitcast, bf16[2048,384]{0,1:T(8,128)(2,1)} %reshape.129), kind=kOutput, calls=%fused_computation.26 | convolution fusion | flops 1611005952 | bytes 6553600 | tf_op jit(solution)/shard_map/dot_general | solution.py:122
  236.4 3.3 all-to-all-done.5
  239.7 3.9 %all-to-all-start.4 = ((bf16[16,64,384]{2,1,0:T(8,128)(2,1)}), bf16[16,64,384]{2,1,0:T(8,128)(2,1)S(1)}, u32[]{:S(2)}, u32[]{:S(2)}) async-start(bf16[16,64,384]{2,1,0:T(8,128)(2,1)} %bitcast.14), calls=%async_computation.5 | async-start | bytes 1572864 | tf_op jit(solution)/shard_map/all_to_all | solution.py:38
  243.9 0.7 convert_reduce_fusion.3
  244.5 14.2 %all-to-all-done.4 = bf16[16,64,384]{2,1,0:T(8,128)(2,1)S(1)} async-done(((bf16[16,64,384]{2,1,0:T(8,128)(2,1)}), bf16[16,64,384]{2,1,0:T(8,128)(2,1)S(1)}, u32[]{:S(2)}, u32[]{:S(2)}) %all-to-all-start.4) | async-done | bytes 786464 | tf_op jit(solution)/shard_map/all_to_all | solution.py:38
  258.8 0.7 convert_reduce_fusion
  259.5 59.2 %reduce-scatter.2.cloned.1.call-done = bf16[256,1024]{1,0:T(8,128)(2,1)} async-done(((bf16[2048,1024]{1,0:T(8,128)(2,1)}), bf16[256,1024]{1,0:T(8,128)(2,1)}) %reduce-scatter.2.cloned.1.call-update) | async-done | bytes 524304 | tf_op jit(solution)/shard_map/reduce_scatter | solution.py:126
  318.7 1.6 fusion.41
  320.3 6.5 %all-reduce.4 = (f32[1024]{0:T(1024)S(1)}, f32[1024]{0:T(1024)S(1)}) all-reduce(f32[1024]{0:T(1024)S(1)} %get-tuple-element.5, f32[1024]{0:T(1024)S(1)} %get-tuple-element.8), channel_id=1, replica_groups=mesh['dp_0'=2,'dp_1'=4,'dp_2'=2,'tensor_0'=4,'tensor_1'=2] {'dp_0'}, use_global_device_ids=true, to_apply=%region_11.12 | all-reduce | flops 2048 | bytes 16384 | tf_op jit(solution)/shard_map/psum | solution.py:43
  326.9 10.5 %all-reduce.1 = (f32[1024]{0:T(1024)S(1)}, f32[1024]{0:T(1024)S(1)}) all-reduce(f32[1024]{0:T(1024)S(1)} %get-tuple-element.17, f32[1024]{0:T(1024)S(1)} %get-tuple-element.18), channel_id=1, replica_groups=mesh['dp_0'=2,'dp_1'=4,'dp_2'=2,'tensor_0'=4,'tensor_1'=2] {'dp_1'}, use_global_device_ids=true, to_apply=%region_12.13 | all-reduce | flops 2048 | bytes 16384 | tf_op jit(solution)/shard_map/psum | solution.py:43
  337.4 2.5 all-reduce.3
  339.9 9.4 %all-reduce = (f32[1024]{0:T(1024)S(1)}, f32[1024]{0:T(1024)S(1)}) all-reduce(f32[1024]{0:T(1024)S(1)} %get-tuple-element.15, f32[1024]{0:T(1024)S(1)} %get-tuple-element.16), channel_id=1, replica_groups=mesh['dp_0'=2,'dp_1'=4,'dp_2'=2,'tensor_0'=4,'tensor_1'=2] {'tensor_0'}, use_global_device_ids=true, to_apply=%region_14.15 | all-reduce | flops 2048 | bytes 16384 | tf_op jit(solution)/shard_map/psum | solution.py:43
  349.3 5.6 %all-reduce.2 = (f32[1024]{0:T(1024)}, f32[1024]{0:T(1024)}) all-reduce(f32[1024]{0:T(1024)S(1)} %get-tuple-element.9, f32[1024]{0:T(1024)S(1)} %get-tuple-element.10), channel_id=1, replica_groups=mesh['dp_0'=2,'dp_1'=4,'dp_2'=2,'tensor_0'=4,'tensor_1'=2] {'tensor_1'}, use_global_device_ids=true, to_apply=%region_15.16 | all-reduce | flops 2048 | bytes 16384 | tf_op jit(solution)/shard_map/psum | solution.py:43
  354.9 2.3 fusion.38
  (30 shorter events, 1.2 us)
Async XLA Ops:
  7.2 36.3 %copy-start.3 = (bf16[256,1024]{1,0:T(8,128)(2,1)S(1)}, bf16[256,1024]{1,0:T(8,128)(2,1)}, u32[]{:S(2)}) copy-start(bf16[256,1024]{1,0:T(8,128)(2,1)} %param.8) | copy-start | bytes 1572868
  45.9 5.6 %copy-start.1 = (bf16[256,1024]{1,0:T(8,128)(2,1)S(1)}, bf16[256,1024]{1,0:T(8,128)(2,1)}, u32[]{:S(2)}) copy-start(bf16[256,1024]{1,0:T(8,128)(2,1)} %param.7) | copy-start | bytes 1572868
  45.9 6.0 %copy-start.4 = (f32[1024]{0:T(1024)S(1)}, f32[1024]{0:T(1024)}, u32[]{:S(2)}) copy-start(f32[1024]{0:T(1024)} %param.10) | copy-start | bytes 12292
  45.9 6.0 %copy-start.5 = (f32[1024]{0:T(1024)S(1)}, f32[1024]{0:T(1024)}, u32[]{:S(2)}) copy-start(f32[1024]{0:T(1024)} %param.11) | copy-start | bytes 12292
  45.9 55.0 %all-to-all-start.2 = ((bf16[8,256,1024]{2,1,0:T(8,128)(2,1)}), bf16[8,256,1024]{2,1,0:T(8,128)(2,1)}, u32[]{:S(2)}, u32[]{:S(2)}) async-start(bf16[8,256,1024]{2,1,0:T(8,128)(2,1)} %broadcast_in_dim.24), calls=%async_computation.2 | async-start | bytes 8388608 | tf_op jit(solution)/shard_map/all_to_all | solution.py:24
  103.5 4.8 %copy-start.6 = (s32[32]{0:T(128)S(1)}, s32[32]{0:T(128)}, u32[]{:S(2)}) copy-start(s32[32]{0:T(128)} %param.9) | copy-start | bytes 388
  103.5 53.2 %all-to-all-start = ((bf16[8,256,1024]{2,1,0:T(8,128)(2,1)}), bf16[8,256,1024]{2,1,0:T(8,128)(2,1)}, u32[]{:S(2)}, u32[]{:S(2)}) async-start(bf16[8,256,1024]{2,1,0:T(8,128)(2,1)} %broadcast_in_dim.16), calls=%async_computation | async-start | bytes 8388608 | tf_op jit(solution)/shard_map/all_to_all | solution.py:24
  108.2 210.6 %reduce-scatter.2.cloned.1.call-start = ((), (), s32[]{:S(2)}) async-start(), calls=%async_computation.7 | async-start | bytes 4718592 | tf_op jit(solution)/shard_map/reduce_scatter | solution.py:126
  111.2 2.0 copy-start
  166.2 12.1 %copy-start.2 = (bf16[32,64,2,64]{1,3,2,0:T(8,128)(2,1)S(1)}, bf16[32,64,2,64]{1,3,2,0:T(8,128)(2,1)}, u32[]{:S(2)}) copy-start(bf16[32,64,2,64]{1,3,2,0:T(8,128)(2,1)} %copy.34) | copy-start | bytes 1572868
  226.0 13.7 %all-to-all-start.5 = ((bf16[16,128,64]{1,2,0:T(8,128)(2,1)}), bf16[16,128,64]{1,2,0:T(8,128)(2,1)S(1)}, u32[]{:S(2)}, u32[]{:S(2)}) async-start(bf16[16,128,64]{1,2,0:T(8,128)(2,1)} %bitcast.17), calls=%async_computation.6 | async-start | bytes 524288 | tf_op jit(solution)/shard_map/all_to_all | solution.py:38
  239.7 19.0 %all-to-all-start.4 = ((bf16[16,64,384]{2,1,0:T(8,128)(2,1)}), bf16[16,64,384]{2,1,0:T(8,128)(2,1)S(1)}, u32[]{:S(2)}, u32[]{:S(2)}) async-start(bf16[16,64,384]{2,1,0:T(8,128)(2,1)} %bitcast.14), calls=%async_computation.5 | async-start | bytes 1572864 | tf_op jit(solution)/shard_map/all_to_all | solution.py:38
Sparse Core Ops, SparseCore 0:
  218.8 99.8 reduce-scatter.1
where the time goes:
time: 365 us; the launch traced here: 364 us
  waiting for transfers between devices  165 us (45%)
  blocking collectives  69.1 us (19%)
  matrix products  45.4 us (12%)
  local copies, waits for them, and re-layouts  40.3 us (11%)
  starting transfers between devices  18.5 us (5%)
  between operations  14.2 us (4%)
  other arithmetic  11.4 us (3%)
    all_to_all x2, waiting for transfers between devices, sent_to_all(): return lax.all_to_all(copies, axis, split_axis=0, concat_axis=0, tiled=True)  88.5 us
    reduce_scatter x1, waiting for transfers between devices, on_device(): lax.psum_scatter(lax.dot_general(grad_proj, qkv_cols, (((1,), (1,)), ((),...  59.2 us
    all_to_all x2, blocking collectives, sent_to_all(): return lax.all_to_all(copies, axis, split_axis=0, concat_axis=0, tiled=True)  34.6 us
    psum x5, blocking collectives, by_axis(): return functools.reduce(lax.psum, axes, value)  34.6 us
    all_to_all x2, waiting for transfers between devices, summed_on_arrival(): lax.all_to_all(pieces, axis, split_axis=0, concat_axis=0, tiled=True)  17.6 us
    slice x1, local copies, waits for them, and re-layouts, on_device(): value_rows = projected[:, :, :, 2]  12.1 us
    all_to_all x2, starting transfers between devices, sent_to_all(): return lax.all_to_all(copies, axis, split_axis=0, concat_axis=0, tiled=True)  10.2 us
    all_to_all x2, starting transfers between devices, summed_on_arrival(): lax.all_to_all(pieces, axis, split_axis=0, concat_axis=0, tiled=True)  8.23 us
  transfers between devices with their start and end apart: 5, of which 5 were waited for; matrix products, arithmetic and copies ran while one was open for 6% of the time, Pallas kernels for 0%

commit v1 on v0

v1 whole, which is shorter than its diff:
```python
import jax
import jax.numpy as jnp
from jax import lax
from jax.experimental import pallas as pl
from jax.experimental.pallas import tpu as pltpu
from jax.sharding import Mesh
from jax.sharding import PartitionSpec as P

HEAD = 64
CAP = 64
MAXC = 49
IMGS = 4
ROWS = 208
MASK_ROW = 200
D = 1024
BLK = 64
WIDE = 512
AXES = ("y_hi", "x", "core", "z", "y_lo")
DP = ("y_hi", "x", "core")
TENSOR = ("z", "y_lo")
PLANE = ("y_lo", "y_hi", "x")
F32 = jnp.float32
BF16 = jnp.bfloat16
VMEM = pl.BlockSpec(memory_space=pltpu.VMEM)
SMEM = pl.BlockSpec(memory_space=pltpu.SMEM)


def ring(n, k):
    return [(i, (i + k) % n) for i in range(n)]


def nn(a, b):
    return lax.dot_general(a, b, (((1,), (0,)), ((), ())), preferred_element_type=F32)


def nt(a, b):
    return lax.dot_general(a, b, (((1,), (1,)), ((), ())), preferred_element_type=F32)


def tn(a, b):
    return lax.dot_general(a, b, (((0,), (0,)), ((), ())), preferred_element_type=F32)


def image_of(index):
    return (
        (index >= MAXC).astype(jnp.int32)
        + (index >= 2 * MAXC).astype(jnp.int32)
        + (index >= 3 * MAXC).astype(jnp.int32)
    )


def count_of(image, counts):
    picked = jnp.where(image == 0, counts[0], counts[1])
    picked = jnp.where(image == 2, counts[2], picked)
    return jnp.where(image == 3, counts[3], picked)


def pack_kernel(start, counts, tokens, upstream, w_qkv, w_out, x_out, u_out, w_cat):
    own = [counts[start[0] + i] for i in range(IMGS)]
    row = lax.broadcasted_iota(jnp.int32, (ROWS, IMGS * CAP), 0)
    col = lax.broadcasted_iota(jnp.int32, (ROWS, IMGS * CAP), 1)
    image = image_of(row)
    slot = row - MAXC * image
    live = slot < count_of(image, own)
    pick = jnp.where(live & (col == CAP * image + slot), 1.0, 0.0).astype(BF16)
    x = nn(pick, tokens[...]).astype(BF16)
    u_out[...] = nn(pick, upstream[...]).astype(BF16)
    key = lax.broadcasted_iota(jnp.int32, (16, D), 1)
    key_image = image_of(key)
    key_slot = key - MAXC * key_image
    key_live = jnp.where(key_slot < count_of(key_image, own), 1.0, 0.0)
    at = lax.broadcasted_iota(jnp.int32, (16, D), 0) == MASK_ROW - (ROWS - 16)
    tail = jnp.where(at, key_live, 0.0).astype(BF16)
    x_out[0 : ROWS - 16] = x[0 : ROWS - 16]
    x_out[ROWS - 16 : ROWS] = x[ROWS - 16 : ROWS] + tail
    for head in range(2):
        for part in range(3):
            w_cat[:, (2 * part + head) * HEAD : (2 * part + head + 1) * HEAD] = w_qkv[
                :, (3 * head + part) * HEAD : (3 * head + part + 1) * HEAD
            ]
    w_cat[:, 6 * HEAD :] = w_out[...].astype(F32).T.astype(BF16)


def block_kernel(
    core, xa, xb, ua, ub, w_own, w_other, gain, bias, g_in, gb_in,
    gn_a, gn_b, g_out, gb_out,
    normed_s, xhat_s, u_s, w_s, *, first, last,
):
    c = core[0]
    for i in range(8):
        w_s[i, c] = w_own[c, i]
        w_s[i, 1 - c] = w_other[c, i]
    gain_row = gain[...]
    bias_row = bias[...]

    for s, (x_ref, u_ref) in enumerate(((xa, ua), (xb, ub))):
        def norm_rows(i, _, x_ref=x_ref, s=s):
            at = pl.multiple_of(i * 16, 16)
            values = x_ref[pl.ds(at, 16), :].astype(F32)
            centre = jnp.mean(values, axis=-1, keepdims=True)
            shifted = values - centre
            variance = jnp.mean(shifted * shifted, axis=-1, keepdims=True)
            scaled = shifted * lax.rsqrt(variance + 1e-06)
            to = pl.multiple_of(s * ROWS + i * 16, 16)
            xhat_s[pl.ds(to, 16), :] = scaled
            normed_s[pl.ds(to, 16), :] = (scaled * gain_row + bias_row).astype(BF16)
            return 0

        lax.fori_loop(0, ROWS // 16, norm_rows, 0)
        u_s[s * ROWS : (s + 1) * ROWS] = u_ref[...]

    weights = w_s[...].reshape(D, WIDE)
    w_proj = weights[:, : 6 * HEAD]
    w_back = weights[:, 6 * HEAD :]
    projected = nn(normed_s[...], w_proj).astype(BF16)
    grad_att = nn(u_s[...], w_back).astype(BF16)

    lane = lax.broadcasted_iota(jnp.int32, (1, 2 * HEAD), 1)
    zero = jnp.zeros((), BF16)
    q_image = jnp.minimum(image_of(lax.broadcasted_iota(jnp.int32, (ROWS, ROWS), 0)), 3)
    key = lax.broadcasted_iota(jnp.int32, (ROWS, ROWS), 1)
    same = (q_image == image_of(key)) & (key < IMGS * MAXC)

    attended_parts = []
    grad_parts = []
    for s, x_ref in enumerate((xa, xb)):
        lo, hi = s * ROWS, (s + 1) * ROWS
        q = projected[lo:hi, 0 : 2 * HEAD]
        k = projected[lo:hi, 2 * HEAD : 4 * HEAD]
        v = projected[lo:hi, 4 * HEAD : 6 * HEAD]
        da = grad_att[lo:hi]
        key_live = x_ref[ROWS - 16 : ROWS, 0:ROWS].astype(F32)[MASK_ROW - (ROWS - 16) : MASK_ROW - (ROWS - 16) + 1]
        keep = same & (key_live > 0.5)
        attended = None
        for head in range(2):
            mine = (lane < HEAD) if head == 0 else (lane >= HEAD)
            q_h = jnp.where(mine, q, zero)
            k_h = jnp.where(mine, k, zero)
            v_h = jnp.where(mine, v, zero)
            da_h = jnp.where(mine, da, zero)
            scores = jnp.where(keep, nt(q_h, k) * (1.0 / 8.0), -1e30)
            top = jnp.max(scores, axis=-1, keepdims=True)
            powers = jnp.exp(scores - top)
            probs = powers / jnp.sum(powers, axis=-1, keepdims=True)
            low = probs.astype(BF16)
            grad_probs = nt(da_h, v)
            delta = jnp.sum(probs * grad_probs, axis=-1, keepdims=True)
            grad_scores = (probs * (grad_probs - delta) * (1.0 / 8.0)).astype(BF16)
            att = nn(low, v_h)
            gv = tn(low, da_h)
            gq = nn(grad_scores, k_h)
            gk = tn(grad_scores, q_h)
            if attended is None:
                attended, grad_v, grad_q, grad_k = att, gv, gq, gk
            else:
                attended, grad_v, grad_q, grad_k = attended + att, grad_v + gv, grad_q + gq, grad_k + gk
        attended_parts.append(attended.astype(BF16))
        grad_parts.append(jnp.concatenate([grad_q, grad_k, grad_v], axis=1).astype(BF16))
    attended = jnp.concatenate(attended_parts, axis=0)
    grad_proj = jnp.concatenate(grad_parts, axis=0)

    qkv_part = tn(normed_s[...], grad_proj)
    out_part = tn(u_s[...], attended)
    if not first:
        qkv_part = qkv_part + g_in[:, : 6 * HEAD]
        out_part = out_part + g_in[:, 6 * HEAD :]
    if last:
        for part, at in ((qkv_part, 0), (out_part, 6 * HEAD)):
            part = part.astype(BF16).reshape(8, 2, BLK, -1)
            for half in range(2):
                g_out[half, :, :, at : at + part.shape[-1]] = part[:, half]
    else:
        g_out[:, : 6 * HEAD] = qkv_part
        g_out[:, 6 * HEAD :] = out_part
    grad_normed = nt(grad_proj, w_proj)
    gn_a[...] = grad_normed[:ROWS].astype(BF16)
    gn_b[...] = grad_normed[ROWS:].astype(BF16)
    gain_sum = jnp.sum(grad_normed * xhat_s[...], axis=0, keepdims=True)
    bias_sum = jnp.sum(grad_normed, axis=0, keepdims=True)
    sums = jnp.concatenate([gain_sum, bias_sum], axis=0)
    gb_out[...] = sums if first else gb_in[...] + sums


def finish_kernel(p0, p1, p2, p3, x_ref, u_ref, gain, out):
    grad_normed = (
        p0[...].astype(F32) + p1[...].astype(F32) + p2[...].astype(F32) + p3[...].astype(F32)
    )
    values = x_ref[...].astype(F32)
    centre = jnp.mean(values, axis=-1, keepdims=True)
    shifted = values - centre
    variance = jnp.mean(shifted * shifted, axis=-1, keepdims=True)
    inverse_std = lax.rsqrt(variance + 1e-06)
    scaled = shifted * inverse_std
    g = grad_normed * gain[...]
    grad_ln = inverse_std * (
        g
        - jnp.mean(g, axis=-1, keepdims=True)
        - scaled * jnp.mean(g * scaled, axis=-1, keepdims=True)
    )
    packed = (u_ref[...].astype(F32) + grad_ln).astype(BF16)
    row = lax.broadcasted_iota(jnp.int32, (IMGS * CAP, ROWS), 0)
    col = lax.broadcasted_iota(jnp.int32, (IMGS * CAP, ROWS), 1)
    slot = row % CAP
    pick = jnp.where((slot < MAXC) & (col == MAXC * (row // CAP) + slot), 1.0, 0.0).astype(BF16)
    out[...] = nn(pick, packed).astype(BF16)


def weights_kernel(arrived, qkv_out, out_out):
    total = jnp.sum(arrived[...].astype(F32), axis=0)
    for head in range(2):
        for part in range(3):
            qkv_out[:, (3 * head + part) * HEAD : (3 * head + part + 1) * HEAD] = total[
                :, (2 * part + head) * HEAD : (2 * part + head + 1) * HEAD
            ]
    out_out[...] = total[:, 6 * HEAD :].T


def shape(dims, kind=BF16):
    return jax.ShapeDtypeStruct(dims, kind)


def swap(value):
    return lax.ppermute(value, "core", ring(2, 1))


def on_device(tokens, upstream, counts, norm_gain, norm_bias, w_qkv, w_out):
    core = lax.axis_index("core").astype(jnp.int32).reshape(1)
    start = (lax.axis_index(TENSOR) * IMGS).astype(jnp.int32).reshape(1)
    gain = norm_gain.reshape(1, D)
    bias = norm_bias.reshape(1, D)
    x, u, w_cat = pl.pallas_call(
        pack_kernel,
        in_specs=[SMEM, SMEM, VMEM, VMEM, VMEM, VMEM],
        out_specs=[VMEM, VMEM, VMEM],
        out_shape=[shape((ROWS, D)), shape((ROWS, D)), shape((BLK, WIDE))],
        name="pack",
    )(start, counts, tokens, upstream, w_qkv, w_out)

    xs = [x] + [lax.ppermute(x, "z", ring(4, k)) for k in (1, 2, 3)]
    us = [u] + [lax.ppermute(u, "z", ring(4, k)) for k in (1, 2, 3)]
    copies = jnp.broadcast_to(w_cat, (16, BLK, WIDE))
    w_own = lax.all_to_all(copies, PLANE, 0, 0, tiled=True).reshape(2, 8, BLK, WIDE)
    w_other = swap(w_own)

    order = (0, 1, 3, 2)
    partial = {}
    grads = jnp.zeros((8, 128), F32)
    sums = jnp.zeros((2, D), F32)
    for step, k in enumerate(order):
        first, last = step == 0, step == 3
        g_shape = shape((2, 8, BLK, WIDE)) if last else shape((D, WIDE), F32)

        def kernel(*refs, first=first, last=last):
            block_kernel(*refs, first=first, last=last)

        gn_a, gn_b, grads, sums = pl.pallas_call(
            kernel,
            in_specs=[SMEM] + [VMEM] * 10,
            out_specs=[VMEM] * 4,
            out_shape=[shape((ROWS, D)), shape((ROWS, D)), g_shape, shape((2, D), F32)],
            scratch_shapes=[
                pltpu.VMEM((2 * ROWS, D), BF16),
                pltpu.VMEM((2 * ROWS, D), F32),
                pltpu.VMEM((2 * ROWS, D), BF16),
                pltpu.VMEM((8, 2, BLK, WIDE), BF16),
            ],
            name=f"block{k}",
        )(core, xs[k], swap(xs[k]), us[k], swap(us[k]), w_own, w_other, gain, bias, grads, sums)
        pair = (gn_a.astype(F32) + swap(gn_b).astype(F32)).astype(BF16)
        partial[k] = lax.ppermute(pair, "z", ring(4, 4 - k)) if k else pair

    other = swap(grads)
    here = core[0] == 0
    send = jnp.stack(
        [jnp.where(here, grads[0], other[1]), jnp.where(here, other[0], grads[1])]
    ).reshape(16, BLK, WIDE)
    arrived = lax.all_to_all(send, PLANE, 0, 0, tiled=True)

    for axis, n, k in (
        ("core", 2, 1), ("y_lo", 2, 1), ("z", 4, 2), ("z", 4, 1), ("x", 4, 2), ("x", 4, 1), ("y_hi", 2, 1)
    ):
        sums = sums + lax.ppermute(sums, axis, ring(n, k))

    grad_qkv, grad_out = pl.pallas_call(
        weights_kernel,
        in_specs=[VMEM],
        out_specs=[VMEM, VMEM],
        out_shape=[shape((BLK, 6 * HEAD), F32), shape((2 * HEAD, BLK), F32)],
        name="weights",
    )(arrived)
    grad_tokens = pl.pallas_call(
        finish_kernel,
        in_specs=[VMEM] * 7,
        out_specs=VMEM,
        out_shape=shape((IMGS * CAP, D)),
        name="finish",
    )(partial[0], partial[1], partial[2], partial[3], x, u, gain)
    return (grad_tokens, grad_qkv, grad_out, sums[0], sums[1])


def solution(mesh):
    finer = Mesh(mesh.devices.reshape(2, 4, 2, 4, 2), AXES)
    rows = DP + TENSOR
    in_specs = (P(rows, None), P(rows, None), P(DP), P(), P(), P(DP, TENSOR), P(TENSOR, DP))
    out_specs = (P(rows, None), P(DP, TENSOR), P(TENSOR, DP), P(), P())
    return jax.shard_map(
        on_device, mesh=finer, in_specs=in_specs, out_specs=out_specs, check_vma=False
    )
```

time: 365 us -> 205 us (0.56)
  waiting for transfers between devices: 165 us -> 77.6 us
  blocking collectives: 69.1 us -> 0 us
  Pallas kernels: 0 us -> 59.9 us
  matrix products: 45.4 us -> 0 us
  starting transfers between devices: 18.5 us -> 49.2 us
  local copies, waits for them, and re-layouts: 40.3 us -> 9.81 us
  between operations: 14.2 us -> 0.85 us
  other arithmetic: 11.4 us -> 7.16 us
    all_to_all x4 -> x2, waiting for transfers between devices: 106 us -> 17.6 us  [the longest x1 17.6 us: on_device(): lax.all_to_all(copies, PLANE, 0, 0, tiled=True).reshape(2, 8, BLK, WIDE)]
    ppermute x0 -> x30, waiting for transfers between devices: none -> 60 us  [the longest x7 25.3 us: on_device(): sums = sums + lax.ppermute(sums, axis, ring(n, k))]
    pallas_call x0 -> x7, Pallas kernels: none -> 59.9 us  [the longest x4 51.9 us: on_device(): pl.pallas_call(kernel, in_specs=[SMEM] + [VMEM] * 10, out_specs=[VMEM] *...]
    reduce_scatter x1 -> x0, waiting for transfers between devices: 59.2 us -> none  [on_device(): lax.psum_scatter(lax.dot_general(grad_proj, qkv_cols, (((1,), (1,)), ((),...]
    dot_general x10 -> x0, matrix products: 40.6 us -> none  [the longest x1 6.06 us: on_device(): jnp.einsum('bhqk,bqhe->bkhe', grad_scores, query_rows, preferred_element_...]
    ppermute x0 -> x30, starting transfers between devices: none -> 38.3 us  [the longest x3 18.8 us: on_device(): us = [u] + [lax.ppermute(u, 'z', ring(4, k)) for k in (1, 2, 3)]]
    all_to_all x2 -> x0, blocking collectives: 34.6 us -> none  [sent_to_all(): return lax.all_to_all(copies, axis, split_axis=0, concat_axis=0, tiled=True)]
    psum x5 -> x0, blocking collectives: 34.6 us -> none  [by_axis(): return functools.reduce(lax.psum, axes, value)]
  transfers between devices with their start and end apart: 5 -> 32, of which waited for: 5 -> 13; matrix products, arithmetic and copies ran while one was open for 6% -> 4% of each run, Pallas kernels for 0% -> 21%
where the time goes in v1:
time: 205 us; the launch traced here: 204 us
  waiting for transfers between devices  77.6 us (38%)
  Pallas kernels  59.9 us (29%)
  starting transfers between devices  49.2 us (24%)
  local copies, waits for them, and re-layouts  9.81 us (5%)
  other arithmetic  7.16 us (3%)
    pallas_call x4, Pallas kernels, on_device(): pl.pallas_call(kernel, in_specs=[SMEM] + [VMEM] * 10, out_specs=[VMEM] *...  51.9 us
    ppermute x7, waiting for transfers between devices, on_device(): sums = sums + lax.ppermute(sums, axis, ring(n, k))  25.3 us
    ppermute x3, starting transfers between devices, on_device(): us = [u] + [lax.ppermute(u, 'z', ring(4, k)) for k in (1, 2, 3)]  18.8 us
    all_to_all x1, waiting for transfers between devices, on_device(): lax.all_to_all(copies, PLANE, 0, 0, tiled=True).reshape(2, 8, BLK, WIDE)  17.6 us
    ppermute x3, waiting for transfers between devices, on_device(): partial[k] = lax.ppermute(pair, 'z', ring(4, 4 - k)) if k else pair  14.4 us
    ppermute x3, waiting for transfers between devices, on_device(): us = [u] + [lax.ppermute(u, 'z', ring(4, k)) for k in (1, 2, 3)]  12.4 us
    ppermute x3, waiting for transfers between devices, on_device(): xs = [x] + [lax.ppermute(x, 'z', ring(4, k)) for k in (1, 2, 3)]  7.91 us
    all_to_all x1, starting transfers between devices, on_device(): lax.all_to_all(copies, PLANE, 0, 0, tiled=True).reshape(2, 8, BLK, WIDE)  7.14 us
  transfers between devices with their start and end apart: 32, of which 13 were waited for; matrix products, arithmetic and copies ran while one was open for 4% of the time, Pallas kernels for 21%

profile of v1, /device:TPU:0, one launch (start us, length us, event | category | flops | bytes accessed | tf_op | source)
XLA Modules:
  0.0 204.5 jit_solution(8800316156424418989)
XLA Ops:
  0.6 1.4 copy.12.w_out
  2.1 2.4 %pack.1 = (bf16[208,1024]{1,0:T(8,128)(2,1)}, bf16[208,1024]{1,0:T(8,128)(2,1)}, bf16[64,512]{1,0:T(8,128)(2,1)}) custom-call(s32[1]{0:T(128)} %bitcast.1.start, s32[32]{0:T(128)} %counts.1, bf16[256,1024]{1,0:T(8,128)(2,1)} %tokens.1, bf16[256,1024]{1,0:T(8,128)(2,1)} %upstream.1, bf16[64,384]{1,0:T(8,128)(2,1)} %w_qkv.1, bf16[128,64]{1,0:T(8,128)(2,1)} %copy.12.w_out), custom_call_target="tpu_custom_call" | custom-call | tf_op jit(solution)/shard_map/pack/pallas_call | solution.py:231
  4.5 2.0 broadcast_in_dim.9
  6.5 7.1 %all-to-all-start = ((bf16[16,64,512]{2,1,0:T(8,128)(2,1)}), bf16[16,64,512]{2,1,0:T(8,128)(2,1)S(1)}, u32[]{:S(2)}, u32[]{:S(2)}) async-start(bf16[16,64,512]{2,1,0:T(8,128)(2,1)} %broadcast_in_dim.9), calls=%async_computation | async-start | bytes 2097152 | tf_op jit(solution)/shard_map/all_to_all | solution.py:242
  13.8 17.6 %all-to-all-done = bf16[16,64,512]{2,1,0:T(8,128)(2,1)S(1)} async-done(((bf16[16,64,512]{2,1,0:T(8,128)(2,1)}), bf16[16,64,512]{2,1,0:T(8,128)(2,1)S(1)}, u32[]{:S(2)}, u32[]{:S(2)}) %all-to-all-start) | async-done | bytes 1048608 | tf_op jit(solution)/shard_map/all_to_all | solution.py:242
  31.9 1.9 collective-permute-start.4
  33.8 1.9 collective-permute-start.6
  35.7 1.3 collective-permute-start.14
  37.0 1.6 collective-permute-start.16
  38.7 7.9 %collective-permute-done.4.refs_1_ = bf16[208,1024]{1,0:T(8,128)(2,1)S(1)} collective-permute-done((bf16[208,1024]{1,0:T(8,128)(2,1)S(1)}, bf16[208,1024]{1,0:T(8,128)(2,1)S(1)}, u32[]{:S(2)}, u32[]{:S(2)}) %collective-permute-start.4) | collective-permute-done | bytes 426016 | tf_op jit(solution)/shard_map/ppermute | solution.py:239
  46.6 1.9 collective-permute-start.10
  48.4 6.8 %collective-permute-done.6.refs_3_ = bf16[208,1024]{1,0:T(8,128)(2,1)} collective-permute-done((bf16[208,1024]{1,0:T(8,128)(2,1)S(1)}, bf16[208,1024]{1,0:T(8,128)(2,1)}, u32[]{:S(2)}, u32[]{:S(2)}) %collective-permute-start.6) | collective-permute-done | bytes 426016 | tf_op jit(solution)/shard_map/ppermute | solution.py:240
  55.2 15.3 %collective-permute-start.12 = (bf16[208,1024]{1,0:T(8,128)(2,1)S(1)}, bf16[208,1024]{1,0:T(8,128)(2,1)}, u32[]{:S(2)}, u32[]{:S(2)}) collective-permute-start(bf16[208,1024]{1,0:T(8,128)(2,1)S(1)} %copy-done.4), channel_id=1, source_target_pairs={{0,4},{2,6},{4,0},{6,2},{1,5},{3,7},{5,1},{7,3},{8,12},{10,14},{12... | collective-permute-start | bytes 1277960 | tf_op jit(solution)/shard_map/ppermute | solution.py:240
  71.1 5.6 %collective-permute-done.12.refs_3_ = bf16[208,1024]{1,0:T(8,128)(2,1)} collective-permute-done((bf16[208,1024]{1,0:T(8,128)(2,1)S(1)}, bf16[208,1024]{1,0:T(8,128)(2,1)}, u32[]{:S(2)}, u32[]{:S(2)}) %collective-permute-start.12) | collective-permute-done | bytes 426016 | tf_op jit(solution)/shard_map/ppermute | solution.py:240
  78.0 0.6 broadcast_in_dim.11.refs_10_
  78.6 0.6 broadcast_in_dim.10.refs_9_
  79.2 12.5 %block0.1 = (bf16[208,1024]{1,0:T(8,128)(2,1)}, bf16[208,1024]{1,0:T(8,128)(2,1)}, f32[1024,512]{1,0:T(8,128)}, f32[2,1024]{1,0:T(2,128)}) custom-call(s32[1]{0:T(128)} %bitcast.refs_0_, bf16[208,1024]{1,0:T(8,128)(2,1)} %get-tuple-element.26.refs_1_.x_ref, bf16[208,1024]{1,0:T(8,128)(2,1)} %copy-done.7, bf16[208,1024]{1,0:T(8,128)(2,1)} %get-tuple-element.27.refs_3_.u_ref, ...), custom_call_target="tpu_custom_call" | custom-call | tf_op jit(solution)/shard_map/block0/pallas_call | solution.py:256
  91.7 13.2 %block1.1 = (bf16[208,1024]{1,0:T(8,128)(2,1)}, bf16[208,1024]{1,0:T(8,128)(2,1)}, f32[1024,512]{1,0:T(8,128)}, f32[2,1024]{1,0:T(2,128)}) custom-call(s32[1]{0:T(128)} %bitcast.refs_0_, bf16[208,1024]{1,0:T(8,128)(2,1)} %copy-done.8, bf16[208,1024]{1,0:T(8,128)(2,1)} %copy-done.13, bf16[208,1024]{1,0:T(8,128)(2,1)} %collective-permute-done.6.refs_3_, ...), custom_call_target="tpu_custom_call" | custom-call | tf_op jit(solution)/shard_map/block1/pallas_call | solution.py:256
  104.9 13.1 %block3.1 = (bf16[208,1024]{1,0:T(8,128)(2,1)}, bf16[208,1024]{1,0:T(8,128)(2,1)}, f32[1024,512]{1,0:T(8,128)}, f32[2,1024]{1,0:T(2,128)}) custom-call(s32[1]{0:T(128)} %bitcast.refs_0_, bf16[208,1024]{1,0:T(8,128)(2,1)} %collective-permute-done.14.refs_1_, bf16[208,1024]{1,0:T(8,128)(2,1)} %collective-permute-done.15.refs_2_, ...), custom_call_target="tpu_custom_call" | custom-call | tf_op jit(solution)/shard_map/block3/pallas_call | solution.py:256
  118.1 0.7 copy-done.10
  119.0 13.1 %block2.1 = (bf16[208,1024]{1,0:T(8,128)(2,1)}, bf16[208,1024]{1,0:T(8,128)(2,1)}, bf16[2,8,64,512]{3,2,1,0:T(8,128)(2,1)}, f32[2,1024]{1,0:T(2,128)}) custom-call(s32[1]{0:T(128)} %bitcast.refs_0_, bf16[208,1024]{1,0:T(8,128)(2,1)} %copy-done.6, bf16[208,1024]{1,0:T(8,128)(2,1)} %copy-done.10, bf16[208,1024]{1,0:T(8,128)(2,1)} %collective-permute-done.12.refs_3_, ...), custom_call_target="tpu_custom_call" | custom-call | tf_op jit(solution)/shard_map/block2/pallas_call | solution.py:256
  132.6 2.9 %collective-permute-done.23 = f32[2,1024]{1,0:T(2,128)S(1)} collective-permute-done((f32[2,1024]{1,0:T(2,128)}, f32[2,1024]{1,0:T(2,128)S(1)}, u32[]{:S(2)}, u32[]{:S(2)}) %collective-permute-start.23) | collective-permute-done | bytes 8224 | tf_op jit(solution)/shard_map/ppermute | solution.py:282
  135.5 0.7 add.41
  136.5 3.4 %collective-permute-done.24 = f32[2,1024]{1,0:T(2,128)S(1)} collective-permute-done((f32[2,1024]{1,0:T(2,128)S(1)}, f32[2,1024]{1,0:T(2,128)S(1)}, u32[]{:S(2)}, u32[]{:S(2)}) %collective-permute-start.24) | collective-permute-done | bytes 8224 | tf_op jit(solution)/shard_map/ppermute | solution.py:282
  139.9 3.5 %collective-permute-start.25 = (f32[2,1024]{1,0:T(2,128)S(1)}, f32[2,1024]{1,0:T(2,128)S(1)}, u32[]{:S(2)}, u32[]{:S(2)}) collective-permute-start(f32[2,1024]{1,0:T(2,128)S(1)} %add.42), channel_id=1, source_target_pairs={{0,4},{2,6},{4,0},{6,2},{1,5},{3,7},{5,1},{7,3},{8,12},{10,14},{12... | collective-permute-start | bytes 24584 | tf_op jit(solution)/shard_map/ppermute | solution.py:282
  143.4 1.6 collective-permute-done.25
  145.0 0.9 collective-permute-start.26
  146.0 3.9 %collective-permute-done.26 = f32[2,1024]{1,0:T(2,128)S(1)} collective-permute-done((f32[2,1024]{1,0:T(2,128)S(1)}, f32[2,1024]{1,0:T(2,128)S(1)}, u32[]{:S(2)}, u32[]{:S(2)}) %collective-permute-start.26) | collective-permute-done | bytes 8224 | tf_op jit(solution)/shard_map/ppermute | solution.py:282
  149.9 0.7 collective-permute-start.27
  150.7 4.4 %collective-permute-done.27 = f32[2,1024]{1,0:T(2,128)S(1)} collective-permute-done((f32[2,1024]{1,0:T(2,128)S(1)}, f32[2,1024]{1,0:T(2,128)S(1)}, u32[]{:S(2)}, u32[]{:S(2)}) %collective-permute-start.27) | collective-permute-done | bytes 8224 | tf_op jit(solution)/shard_map/ppermute | solution.py:282
  155.1 4.8 %collective-permute-done.28 = f32[2,1024]{1,0:T(2,128)S(1)} collective-permute-done((f32[2,1024]{1,0:T(2,128)S(1)}, f32[2,1024]{1,0:T(2,128)S(1)}, u32[]{:S(2)}, u32[]{:S(2)}) %collective-permute-start.28) | collective-permute-done | bytes 8224 | tf_op jit(solution)/shard_map/ppermute | solution.py:282
  160.9 4.2 %collective-permute-done.29 = f32[2,1024]{1,0:T(2,128)S(1)} collective-permute-done((f32[2,1024]{1,0:T(2,128)S(1)}, f32[2,1024]{1,0:T(2,128)S(1)}, u32[]{:S(2)}, u32[]{:S(2)}) %collective-permute-start.29) | collective-permute-done | bytes 8224 | tf_op jit(solution)/shard_map/ppermute | solution.py:282
  165.1 0.9 add_convert_fusion
  166.2 1.1 pad_maximum_fusion
  167.3 3.8 %all-to-all-start.1 = ((bf16[16,64,512]{2,1,0:T(8,128)(2,1)}), bf16[16,64,512]{2,1,0:T(8,128)(2,1)S(1)}, u32[]{:S(2)}, u32[]{:S(2)}) async-start(bf16[16,64,512]{2,1,0:T(8,128)(2,1)} %bitcast.5), calls=%async_computation.1 | async-start | bytes 2097152 | tf_op jit(solution)/shard_map/all_to_all | solution.py:277
  171.1 1.2 add_convert_fusion.1
  172.3 2.4 %collective-permute-start.19 = (bf16[208,1024]{1,0:T(8,128)(2,1)S(1)}, bf16[208,1024]{1,0:T(8,128)(2,1)S(1)}, u32[]{:S(2)}, u32[]{:S(2)}) collective-permute-start(bf16[208,1024]{1,0:T(8,128)(2,1)S(1)} %add_convert_fusion.1), channel_id=1, source_target_pairs={{0,4},{2,6},{4,0},{6,2},{1,5},{3,7},{5,1},{7,3},{8,12},{10,14},{12... | collective-permute-start | bytes 1277960 | tf_op jit(solution)/shard_map/ppermute | solution.py:270
  174.7 1.2 add_convert_fusion.2
  175.8 2.7 %collective-permute-start.9 = (bf16[208,1024]{1,0:T(8,128)(2,1)S(1)}, bf16[208,1024]{1,0:T(8,128)(2,1)S(1)}, u32[]{:S(2)}, u32[]{:S(2)}) collective-permute-start(bf16[208,1024]{1,0:T(8,128)(2,1)S(1)} %add_convert_fusion.2), channel_id=1, source_target_pairs={{0,6},{2,0},{4,2},{6,4},{1,7},{3,1},{5,3},{7,5},{8,14},{10,8},{12,... | collective-permute-start | bytes 1277960 | tf_op jit(solution)/shard_map/ppermute | solution.py:270
  178.5 0.6 fusion
  179.1 2.0 add_convert_fusion.3.p0
  181.1 7.7 %collective-permute-done.21.p3 = bf16[208,1024]{1,0:T(8,128)(2,1)S(1)} collective-permute-done((bf16[208,1024]{1,0:T(8,128)(2,1)}, bf16[208,1024]{1,0:T(8,128)(2,1)S(1)}, u32[]{:S(2)}, u32[]{:S(2)}) %collective-permute-start.21) | collective-permute-done | bytes 426016 | tf_op jit(solution)/shard_map/ppermute | solution.py:270
  188.8 6.7 %collective-permute-done.9.p1 = bf16[208,1024]{1,0:T(8,128)(2,1)S(1)} collective-permute-done((bf16[208,1024]{1,0:T(8,128)(2,1)S(1)}, bf16[208,1024]{1,0:T(8,128)(2,1)S(1)}, u32[]{:S(2)}, u32[]{:S(2)}) %collective-permute-start.9) | collective-permute-done | bytes 426016 | tf_op jit(solution)/shard_map/ppermute | solution.py:270
  195.5 0.8 copy-done.15
  196.3 3.5 %finish.1 = bf16[256,1024]{1,0:T(8,128)(2,1)} custom-call(bf16[208,1024]{1,0:T(8,128)(2,1)} %add_convert_fusion.3.p0, bf16[208,1024]{1,0:T(8,128)(2,1)} %copy-done.15, bf16[208,1024]{1,0:T(8,128)(2,1)} %copy-done.14, bf16[208,1024]{1,0:T(8,128)(2,1)} %copy-done.11, bf16[208,1024]{1,0:T(8,128)(2,1)} %get-tuple-element.26.refs_1_.x_ref, ...), custom_call_target="tpu_custom_call" | custom-call | tf_op jit(solution)/shard_map/finish/pallas_call | solution.py:291
  199.8 1.0 copy-done.2
  200.8 2.1 %weights.1 = (f32[64,384]{1,0:T(8,128)}, f32[128,64]{1,0:T(8,128)}) custom-call(bf16[16,64,512]{2,1,0:T(8,128)(2,1)} %copy-done.2), custom_call_target="tpu_custom_call" | custom-call | tf_op jit(solution)/shard_map/weights/pallas_call | solution.py:284
  202.9 1.5 copy.13
  (82 shorter events, 4.7 us)
Async XLA Ops:
  4.5 9.2 %copy-start.3 = (bf16[208,1024]{1,0:T(8,128)(2,1)S(1)}, bf16[208,1024]{1,0:T(8,128)(2,1)}, u32[]{:S(2)}) copy-start(bf16[208,1024]{1,0:T(8,128)(2,1)} %get-tuple-element.26.refs_1_.x_ref) | copy-start | bytes 1277956
  4.5 26.9 %copy-start.4 = (bf16[208,1024]{1,0:T(8,128)(2,1)S(1)}, bf16[208,1024]{1,0:T(8,128)(2,1)}, u32[]{:S(2)}) copy-start(bf16[208,1024]{1,0:T(8,128)(2,1)} %get-tuple-element.27.refs_3_.u_ref) | copy-start | bytes 1277956
  6.5 24.8 %all-to-all-start = ((bf16[16,64,512]{2,1,0:T(8,128)(2,1)}), bf16[16,64,512]{2,1,0:T(8,128)(2,1)S(1)}, u32[]{:S(2)}, u32[]{:S(2)}) async-start(bf16[16,64,512]{2,1,0:T(8,128)(2,1)} %broadcast_in_dim.9), calls=%async_computation | async-start | bytes 2097152 | tf_op jit(solution)/shard_map/all_to_all | solution.py:242
  13.7 22.0 %collective-permute-start = (bf16[208,1024]{1,0:T(8,128)(2,1)S(1)}, bf16[208,1024]{1,0:T(8,128)(2,1)S(1)}, u32[]{:S(2)}, u32[]{:S(2)}) collective-permute-start(bf16[208,1024]{1,0:T(8,128)(2,1)S(1)} %copy-done.3), channel_id=1, source_target_pairs={{0,8},{8,0},{1,9},{9,1},{2,10},{10,2},{3,11},{11,3},{4,12},{12,4},... | collective-permute-start | bytes 1277960 | tf_op jit(solution)/shard_map/ppermute | solution.py:223
  31.4 47.8 %copy-start = (bf16[16,64,512]{2,1,0:T(8,128)(2,1)}, bf16[16,64,512]{2,1,0:T(8,128)(2,1)S(1)}, u32[]{:S(2)}) copy-start(bf16[16,64,512]{2,1,0:T(8,128)(2,1)S(1)} %all-to-all-done) | copy-start | bytes 3145732
  31.4 45.9 %collective-permute-start.2 = (bf16[2,8,64,512]{3,2,1,0:T(8,128)(2,1)S(1)}, bf16[2,8,64,512]{3,2,1,0:T(8,128)(2,1)S(1)}, u32[]{:S(2)}, u32[]{:S(2)}) collective-permute-start(bf16[2,8,64,512]{3,2,1,0:T(8,128)(2,1)S(1)} %bitcast.8), channel_id=1, source_target_pairs={{0,8},{8,0},{1,9},{9,1},{2,10},{10,2},{3,11},{11,3},{4,12},{12,4},... | collective-permute-start | bytes 3145736 | tf_op jit(solution)/shard_map/ppermute | solution.py:223
  31.4 5.7 %collective-permute-start.1 = (bf16[208,1024]{1,0:T(8,128)(2,1)S(1)}, bf16[208,1024]{1,0:T(8,128)(2,1)S(1)}, u32[]{:S(2)}, u32[]{:S(2)}) collective-permute-start(bf16[208,1024]{1,0:T(8,128)(2,1)S(1)} %copy-done.4), channel_id=1, source_target_pairs={{0,8},{8,0},{1,9},{9,1},{2,10},{10,2},{3,11},{11,3},{4,12},{12,4},... | collective-permute-start | bytes 1277960 | tf_op jit(solution)/shard_map/ppermute | solution.py:223
  31.9 14.7 %collective-permute-start.4 = (bf16[208,1024]{1,0:T(8,128)(2,1)S(1)}, bf16[208,1024]{1,0:T(8,128)(2,1)S(1)}, u32[]{:S(2)}, u32[]{:S(2)}) collective-permute-start(bf16[208,1024]{1,0:T(8,128)(2,1)S(1)} %copy-done.3), channel_id=1, source_target_pairs={{0,2},{2,4},{4,6},{6,0},{1,3},{3,5},{5,7},{7,1},{8,10},{10,12},{12... | collective-permute-start | bytes 1277960 | tf_op jit(solution)/shard_map/ppermute | solution.py:239
  33.8 21.4 %collective-permute-start.6 = (bf16[208,1024]{1,0:T(8,128)(2,1)S(1)}, bf16[208,1024]{1,0:T(8,128)(2,1)}, u32[]{:S(2)}, u32[]{:S(2)}) collective-permute-start(bf16[208,1024]{1,0:T(8,128)(2,1)S(1)} %copy-done.4), channel_id=1, source_target_pairs={{0,2},{2,4},{4,6},{6,0},{1,3},{3,5},{5,7},{7,1},{8,10},{10,12},{12... | collective-permute-start | bytes 1277960 | tf_op jit(solution)/shard_map/ppermute | solution.py:240
  35.7 3.0 %copy-start.7 = (bf16[208,1024]{1,0:T(8,128)(2,1)}, bf16[208,1024]{1,0:T(8,128)(2,1)S(1)}, u32[]{:S(2)}) copy-start(bf16[208,1024]{1,0:T(8,128)(2,1)S(1)} %collective-permute-done.refs_2_) | copy-start | bytes 1277956
  35.7 34.8 %collective-permute-start.14 = (bf16[208,1024]{1,0:T(8,128)(2,1)S(1)}, bf16[208,1024]{1,0:T(8,128)(2,1)}, u32[]{:S(2)}, u32[]{:S(2)}) collective-permute-start(bf16[208,1024]{1,0:T(8,128)(2,1)S(1)} %copy-done.3), channel_id=1, source_target_pairs={{0,6},{2,0},{4,2},{6,4},{1,7},{3,1},{5,3},{7,5},{8,14},{10,8},{12,... | collective-permute-start | bytes 1277960 | tf_op jit(solution)/shard_map/ppermute | solution.py:239
  37.0 40.2 %copy-start.9 = (bf16[208,1024]{1,0:T(8,128)(2,1)}, bf16[208,1024]{1,0:T(8,128)(2,1)S(1)}, u32[]{:S(2)}) copy-start(bf16[208,1024]{1,0:T(8,128)(2,1)S(1)} %collective-permute-done.1.refs_4_) | copy-start | bytes 1277956
  37.0 33.5 %collective-permute-start.16 = (bf16[208,1024]{1,0:T(8,128)(2,1)S(1)}, bf16[208,1024]{1,0:T(8,128)(2,1)}, u32[]{:S(2)}, u32[]{:S(2)}) collective-permute-start(bf16[208,1024]{1,0:T(8,128)(2,1)S(1)} %copy-done.4), channel_id=1, source_target_pairs={{0,6},{2,0},{4,2},{6,4},{1,7},{3,1},{5,3},{7,5},{8,14},{10,8},{12,... | collective-permute-start | bytes 1277960 | tf_op jit(solution)/shard_map/ppermute | solution.py:240
  46.6 30.6 %copy-start.8 = (bf16[208,1024]{1,0:T(8,128)(2,1)}, bf16[208,1024]{1,0:T(8,128)(2,1)S(1)}, u32[]{:S(2)}) copy-start(bf16[208,1024]{1,0:T(8,128)(2,1)S(1)} %collective-permute-done.4.refs_1_) | copy-start | bytes 1277956
  46.6 24.4 %collective-permute-start.10 = (bf16[208,1024]{1,0:T(8,128)(2,1)S(1)}, bf16[208,1024]{1,0:T(8,128)(2,1)S(1)}, u32[]{:S(2)}, u32[]{:S(2)}) collective-permute-start(bf16[208,1024]{1,0:T(8,128)(2,1)S(1)} %copy-done.3), channel_id=1, source_target_pairs={{0,4},{2,6},{4,0},{6,2},{1,5},{3,7},{5,1},{7,3},{8,12},{10,14},{12... | collective-permute-start | bytes 1277960 | tf_op jit(solution)/shard_map/ppermute | solution.py:239
  55.2 21.5 %collective-permute-start.12 = (bf16[208,1024]{1,0:T(8,128)(2,1)S(1)}, bf16[208,1024]{1,0:T(8,128)(2,1)}, u32[]{:S(2)}, u32[]{:S(2)}) collective-permute-start(bf16[208,1024]{1,0:T(8,128)(2,1)S(1)} %copy-done.4), channel_id=1, source_target_pairs={{0,4},{2,6},{4,0},{6,2},{1,5},{3,7},{5,1},{7,3},{8,12},{10,14},{12... | collective-permute-start | bytes 1277960 | tf_op jit(solution)/shard_map/ppermute | solution.py:240
  70.5 6.2 %collective-permute-start.5 = (bf16[208,1024]{1,0:T(8,128)(2,1)S(1)}, bf16[208,1024]{1,0:T(8,128)(2,1)S(1)}, u32[]{:S(2)}, u32[]{:S(2)}) collective-permute-start(bf16[208,1024]{1,0:T(8,128)(2,1)S(1)} %collective-permute-done.4.refs_1_), channel_id=1, source_target_pairs={{0,8},{8,0},{1,9},{9,1},{2,10},{10,2},{3,11},{11,3},{4,12},{12,4},... | collective-permute-start | bytes 1277960 | tf_op jit(solution)/shard_map/ppermute | solution.py:223
  70.5 21.2 %collective-permute-start.7 = (bf16[208,1024]{1,0:T(8,128)(2,1)}, bf16[208,1024]{1,0:T(8,128)(2,1)}, u32[]{:S(2)}, u32[]{:S(2)}) collective-permute-start(bf16[208,1024]{1,0:T(8,128)(2,1)} %collective-permute-done.6.refs_3_), channel_id=1, source_target_pairs={{0,8},{8,0},{1,9},{9,1},{2,10},{10,2},{3,11},{11,3},{4,12},{12,4},... | collective-permute-start | bytes 1277960 | tf_op jit(solution)/shard_map/ppermute | solution.py:223
  71.0 47.0 %copy-start.6 = (bf16[208,1024]{1,0:T(8,128)(2,1)}, bf16[208,1024]{1,0:T(8,128)(2,1)S(1)}, u32[]{:S(2)}) copy-start(bf16[208,1024]{1,0:T(8,128)(2,1)S(1)} %collective-permute-done.10.refs_1_) | copy-start | bytes 1277956
  71.0 33.9 %collective-permute-start.15 = (bf16[208,1024]{1,0:T(8,128)(2,1)}, bf16[208,1024]{1,0:T(8,128)(2,1)}, u32[]{:S(2)}, u32[]{:S(2)}) collective-permute-start(bf16[208,1024]{1,0:T(8,128)(2,1)} %collective-permute-done.14.refs_1_), channel_id=1, source_target_pairs={{0,8},{8,0},{1,9},{9,1},{2,10},{10,2},{3,11},{11,3},{4,12},{12,4},... | collective-permute-start | bytes 1277960 | tf_op jit(solution)/shard_map/ppermute | solution.py:223
  76.7 28.2 %collective-permute-start.17 = (bf16[208,1024]{1,0:T(8,128)(2,1)}, bf16[208,1024]{1,0:T(8,128)(2,1)}, u32[]{:S(2)}, u32[]{:S(2)}) collective-permute-start(bf16[208,1024]{1,0:T(8,128)(2,1)} %collective-permute-done.16.refs_3_), channel_id=1, source_target_pairs={{0,8},{8,0},{1,9},{9,1},{2,10},{10,2},{3,11},{11,3},{4,12},{12,4},... | collective-permute-start | bytes 1277960 | tf_op jit(solution)/shard_map/ppermute | solution.py:223
  76.7 41.3 %collective-permute-start.11 = (bf16[208,1024]{1,0:T(8,128)(2,1)S(1)}, bf16[208,1024]{1,0:T(8,128)(2,1)S(1)}, u32[]{:S(2)}, u32[]{:S(2)}) collective-permute-start(bf16[208,1024]{1,0:T(8,128)(2,1)S(1)} %collective-permute-done.10.refs_1_), channel_id=1, source_target_pairs={{0,8},{8,0},{1,9},{9,1},{2,10},{10,2},{3,11},{11,3},{4,12},{12,4},... | collective-permute-start | bytes 1277960 | tf_op jit(solution)/shard_map/ppermute | solution.py:223
  77.5 1.7 copy-start.1
  77.5 40.6 %collective-permute-start.13 = (bf16[208,1024]{1,0:T(8,128)(2,1)}, bf16[208,1024]{1,0:T(8,128)(2,1)S(1)}, u32[]{:S(2)}, u32[]{:S(2)}) collective-permute-start(bf16[208,1024]{1,0:T(8,128)(2,1)} %collective-permute-done.12.refs_3_), channel_id=1, source_target_pairs={{0,8},{8,0},{1,9},{9,1},{2,10},{10,2},{3,11},{11,3},{4,12},{12,4},... | collective-permute-start | bytes 1277960 | tf_op jit(solution)/shard_map/ppermute | solution.py:223
  118.9 46.2 %copy-start.19 = (bf16[208,1024]{1,0:T(8,128)(2,1)S(1)}, bf16[208,1024]{1,0:T(8,128)(2,1)}, u32[]{:S(2)}) copy-start(bf16[208,1024]{1,0:T(8,128)(2,1)} %get-tuple-element.41) | copy-start | bytes 1277956
  132.0 34.0 %copy-start.5 = (bf16[2,8,64,512]{3,2,1,0:T(8,128)(2,1)S(1)}, bf16[2,8,64,512]{3,2,1,0:T(8,128)(2,1)}, u32[]{:S(2)}) copy-start(bf16[2,8,64,512]{3,2,1,0:T(8,128)(2,1)} %get-tuple-element.43) | copy-start | bytes 3145732
  132.0 34.0 %collective-permute-start.22 = (bf16[2,8,64,512]{3,2,1,0:T(8,128)(2,1)}, bf16[2,8,64,512]{3,2,1,0:T(8,128)(2,1)S(1)}, u32[]{:S(2)}, u32[]{:S(2)}) collective-permute-start(bf16[2,8,64,512]{3,2,1,0:T(8,128)(2,1)} %get-tuple-element.43), channel_id=1, source_target_pairs={{0,8},{8,0},{1,9},{9,1},{2,10},{10,2},{3,11},{11,3},{4,12},{12,4},... | collective-permute-start | bytes 3145736 | tf_op jit(solution)/shard_map/ppermute | solution.py:223
  132.1 33.0 %collective-permute-start.20 = (bf16[208,1024]{1,0:T(8,128)(2,1)}, bf16[208,1024]{1,0:T(8,128)(2,1)S(1)}, u32[]{:S(2)}, u32[]{:S(2)}) collective-permute-start(bf16[208,1024]{1,0:T(8,128)(2,1)} %get-tuple-element.42), channel_id=1, source_target_pairs={{0,8},{8,0},{1,9},{9,1},{2,10},{10,2},{3,11},{11,3},{4,12},{12,4},... | collective-permute-start | bytes 1277960 | tf_op jit(solution)/shard_map/ppermute | solution.py:223
  132.5 3.0 %collective-permute-start.23 = (f32[2,1024]{1,0:T(2,128)}, f32[2,1024]{1,0:T(2,128)S(1)}, u32[]{:S(2)}, u32[]{:S(2)}) collective-permute-start(f32[2,1024]{1,0:T(2,128)} %get-tuple-element.46), channel_id=1, source_target_pairs={{0,8},{8,0},{1,9},{9,1},{2,10},{10,2},{3,11},{11,3},{4,12},{12,4},... | collective-permute-start | bytes 24584 | tf_op jit(solution)/shard_map/ppermute | solution.py:282
  136.2 3.7 %collective-permute-start.24 = (f32[2,1024]{1,0:T(2,128)S(1)}, f32[2,1024]{1,0:T(2,128)S(1)}, u32[]{:S(2)}, u32[]{:S(2)}) collective-permute-start(f32[2,1024]{1,0:T(2,128)S(1)} %add.41), channel_id=1, source_target_pairs={{0,1},{1,0},{2,3},{3,2},{4,5},{5,4},{6,7},{7,6},{8,9},{9,8},{10,11... | collective-permute-start | bytes 24584 | tf_op jit(solution)/shard_map/ppermute | solution.py:282
  139.9 5.2 %collective-permute-start.25 = (f32[2,1024]{1,0:T(2,128)S(1)}, f32[2,1024]{1,0:T(2,128)S(1)}, u32[]{:S(2)}, u32[]{:S(2)}) collective-permute-start(f32[2,1024]{1,0:T(2,128)S(1)} %add.42), channel_id=1, source_target_pairs={{0,4},{2,6},{4,0},{6,2},{1,5},{3,7},{5,1},{7,3},{8,12},{10,14},{12... | collective-permute-start | bytes 24584 | tf_op jit(solution)/shard_map/ppermute | solution.py:282
  145.0 4.9 %collective-permute-start.26 = (f32[2,1024]{1,0:T(2,128)S(1)}, f32[2,1024]{1,0:T(2,128)S(1)}, u32[]{:S(2)}, u32[]{:S(2)}) collective-permute-start(f32[2,1024]{1,0:T(2,128)S(1)} %add.43), channel_id=1, source_target_pairs={{0,2},{2,4},{4,6},{6,0},{1,3},{3,5},{5,7},{7,1},{8,10},{10,12},{12... | collective-permute-start | bytes 24584 | tf_op jit(solution)/shard_map/ppermute | solution.py:282
  149.9 5.2 %collective-permute-start.27 = (f32[2,1024]{1,0:T(2,128)S(1)}, f32[2,1024]{1,0:T(2,128)S(1)}, u32[]{:S(2)}, u32[]{:S(2)}) collective-permute-start(f32[2,1024]{1,0:T(2,128)S(1)} %add.44), channel_id=1, source_target_pairs={{0,32},{16,48},{32,0},{48,16},{1,33},{17,49},{33,1},{49,17},{2,34}... | collective-permute-start | bytes 24584 | tf_op jit(solution)/shard_map/ppermute | solution.py:282
  155.1 4.9 %collective-permute-start.28 = (f32[2,1024]{1,0:T(2,128)S(1)}, f32[2,1024]{1,0:T(2,128)S(1)}, u32[]{:S(2)}, u32[]{:S(2)}) collective-permute-start(f32[2,1024]{1,0:T(2,128)S(1)} %add.45), channel_id=1, source_target_pairs={{0,16},{16,32},{32,48},{48,0},{1,17},{17,33},{33,49},{49,1},{2,18}... | collective-permute-start | bytes 24584 | tf_op jit(solution)/shard_map/ppermute | solution.py:282
  159.9 5.2 %collective-permute-start.29 = (f32[2,1024]{1,0:T(2,128)S(1)}, f32[2,1024]{1,0:T(2,128)S(1)}, u32[]{:S(2)}, u32[]{:S(2)}) collective-permute-start(f32[2,1024]{1,0:T(2,128)S(1)} %add.46), channel_id=1, source_target_pairs={{0,64},{64,0},{1,65},{65,1},{2,66},{66,2},{3,67},{67,3},{4,68},{68... | collective-permute-start | bytes 24584 | tf_op jit(solution)/shard_map/ppermute | solution.py:282
  160.4 10.7 %collective-permute-start.18 = (bf16[208,1024]{1,0:T(8,128)(2,1)}, bf16[208,1024]{1,0:T(8,128)(2,1)}, u32[]{:S(2)}, u32[]{:S(2)}) collective-permute-start(bf16[208,1024]{1,0:T(8,128)(2,1)} %get-tuple-element.40), channel_id=1, source_target_pairs={{0,8},{8,0},{1,9},{9,1},{2,10},{10,2},{3,11},{11,3},{4,12},{12,4},... | collective-permute-start | bytes 1277960 | tf_op jit(solution)/shard_map/ppermute | solution.py:223
  160.4 14.3 %collective-permute-start.8 = (bf16[208,1024]{1,0:T(8,128)(2,1)}, bf16[208,1024]{1,0:T(8,128)(2,1)}, u32[]{:S(2)}, u32[]{:S(2)}) collective-permute-start(bf16[208,1024]{1,0:T(8,128)(2,1)} %get-tuple-element.34), channel_id=1, source_target_pairs={{0,8},{8,0},{1,9},{9,1},{2,10},{10,2},{3,11},{11,3},{4,12},{12,4},... | collective-permute-start | bytes 1277960 | tf_op jit(solution)/shard_map/ppermute | solution.py:223
  165.1 14.0 %collective-permute-start.3 = (bf16[208,1024]{1,0:T(8,128)(2,1)}, bf16[208,1024]{1,0:T(8,128)(2,1)}, u32[]{:S(2)}, u32[]{:S(2)}) collective-permute-start(bf16[208,1024]{1,0:T(8,128)(2,1)} %get-tuple-element.30), channel_id=1, source_target_pairs={{0,8},{8,0},{1,9},{9,1},{2,10},{10,2},{3,11},{11,3},{4,12},{12,4},... | collective-permute-start | bytes 1277960 | tf_op jit(solution)/shard_map/ppermute | solution.py:223
  166.0 22.8 %collective-permute-start.21 = (bf16[208,1024]{1,0:T(8,128)(2,1)}, bf16[208,1024]{1,0:T(8,128)(2,1)S(1)}, u32[]{:S(2)}, u32[]{:S(2)}) collective-permute-start(bf16[208,1024]{1,0:T(8,128)(2,1)} %add_convert_fusion), channel_id=1, source_target_pairs={{0,2},{2,4},{4,6},{6,0},{1,3},{3,5},{5,7},{7,1},{8,10},{10,12},{12... | collective-permute-start | bytes 1277960 | tf_op jit(solution)/shard_map/ppermute | solution.py:270
  166.2 4.9 %copy-start.18 = (bf16[208,1024]{1,0:T(8,128)(2,1)S(1)}, bf16[208,1024]{1,0:T(8,128)(2,1)}, u32[]{:S(2)}) copy-start(bf16[208,1024]{1,0:T(8,128)(2,1)} %get-tuple-element.39) | copy-start | bytes 1277956
  167.3 7.4 %copy-start.17 = (bf16[208,1024]{1,0:T(8,128)(2,1)S(1)}, bf16[208,1024]{1,0:T(8,128)(2,1)}, u32[]{:S(2)}) copy-start(bf16[208,1024]{1,0:T(8,128)(2,1)} %get-tuple-element.33) | copy-start | bytes 1277956
  167.3 11.8 %copy-start.16 = (bf16[208,1024]{1,0:T(8,128)(2,1)S(1)}, bf16[208,1024]{1,0:T(8,128)(2,1)}, u32[]{:S(2)}) copy-start(bf16[208,1024]{1,0:T(8,128)(2,1)} %get-tuple-element.29) | copy-start | bytes 1277956
  167.3 32.5 %all-to-all-start.1 = ((bf16[16,64,512]{2,1,0:T(8,128)(2,1)}), bf16[16,64,512]{2,1,0:T(8,128)(2,1)S(1)}, u32[]{:S(2)}, u32[]{:S(2)}) async-start(bf16[16,64,512]{2,1,0:T(8,128)(2,1)} %bitcast.5), calls=%async_computation.1 | async-start | bytes 2097152 | tf_op jit(solution)/shard_map/all_to_all | solution.py:277
  172.3 16.5 %collective-permute-start.19 = (bf16[208,1024]{1,0:T(8,128)(2,1)S(1)}, bf16[208,1024]{1,0:T(8,128)(2,1)S(1)}, u32[]{:S(2)}, u32[]{:S(2)}) collective-permute-start(bf16[208,1024]{1,0:T(8,128)(2,1)S(1)} %add_convert_fusion.1), channel_id=1, source_target_pairs={{0,4},{2,6},{4,0},{6,2},{1,5},{3,7},{5,1},{7,3},{8,12},{10,14},{12... | collective-permute-start | bytes 1277960 | tf_op jit(solution)/shard_map/ppermute | solution.py:270
  175.8 19.7 %collective-permute-start.9 = (bf16[208,1024]{1,0:T(8,128)(2,1)S(1)}, bf16[208,1024]{1,0:T(8,128)(2,1)S(1)}, u32[]{:S(2)}, u32[]{:S(2)}) collective-permute-start(bf16[208,1024]{1,0:T(8,128)(2,1)S(1)} %add_convert_fusion.2), channel_id=1, source_target_pairs={{0,6},{2,0},{4,2},{6,4},{1,7},{3,1},{5,3},{7,5},{8,14},{10,8},{12,... | collective-permute-start | bytes 1277960 | tf_op jit(solution)/shard_map/ppermute | solution.py:270
  188.8 6.7 %copy-start.11 = (bf16[208,1024]{1,0:T(8,128)(2,1)}, bf16[208,1024]{1,0:T(8,128)(2,1)S(1)}, u32[]{:S(2)}) copy-start(bf16[208,1024]{1,0:T(8,128)(2,1)S(1)} %collective-permute-done.21.p3) | copy-start | bytes 1277956
  188.8 6.7 %copy-start.14 = (bf16[208,1024]{1,0:T(8,128)(2,1)}, bf16[208,1024]{1,0:T(8,128)(2,1)S(1)}, u32[]{:S(2)}) copy-start(bf16[208,1024]{1,0:T(8,128)(2,1)S(1)} %collective-permute-done.19.p2) | copy-start | bytes 1277956
  199.8 1.0 copy-start.2
  (4 other events, 3.2 us)
